TPU v7x, 16 devices: a whole 2x2x2 slice. The times are simulated.
16 devices in a mesh: fsdp: 16 (over z, y, x, core).
Axes of the slice: x: 2, y: 2, z: 2, core: 2. Of those that a mesh axis runs over, the one named last changes fastest.
Arguments:
- tokens: int32 [16, 256], P('fsdp')
- embed_table: float32 [151936, 896], P('fsdp')
- norm_gain: float32 [896], P('fsdp')
- w_query: float32 [896, 896], P('fsdp')
- w_key: float32 [896, 128], P('fsdp')
- w_value: float32 [896, 128], P('fsdp')
- d_query: bfloat16 [16, 256, 896], P('fsdp')
- d_key: bfloat16 [16, 256, 128], P('fsdp')
- d_value: bfloat16 [16, 256, 128], P('fsdp')
Outputs:
- output 1: bfloat16 [16, 256, 896], P('fsdp')
- output 2: bfloat16 [16, 256, 128], P('fsdp')
- output 3: bfloat16 [16, 256, 128], P('fsdp')
- output 4: float32 [151936, 896], P('fsdp')
- output 5: float32 [896], P('fsdp')
- output 6: float32 [896, 896], P('fsdp')
- output 7: float32 [896, 128], P('fsdp')
- output 8: float32 [896, 128], P('fsdp')
All inputs are finite; a program needn't handle non-finite values.
Results may differ from a plain program's by a relative error of at most 0.00452988.
Values are sent between devices in bfloat16 or wider.
A program may use at most 1 GiB of HBM per device.

v0:
```python
import jax
import jax.numpy as jnp
from jax import lax
from jax.sharding import PartitionSpec as P

AXIS_NAME = "fsdp"


def norm_forward(x_rows, gain_full):
    inv_rms = lax.rsqrt(jnp.mean(x_rows * x_rows, axis=-1, keepdims=True) + 1e-5)
    h_rows = x_rows * inv_rms
    return inv_rms, h_rows, (h_rows * gain_full).astype(jnp.bfloat16)


def solution(mesh):
    def local_step(tokens, embed_shard, gain_shard, wq_shard, wk_shard, wv_shard, d_query, d_key, d_value):
        vocab_local = embed_shard.shape[0]
        dev_index = lax.axis_index(AXIS_NAME)
        all_tokens = lax.all_gather(tokens, AXIS_NAME, axis=0, tiled=True)
        local_ids = all_tokens - dev_index * vocab_local
        is_owned = (local_ids >= 0) & (local_ids < vocab_local)
        owned_rows = jnp.take(embed_shard, jnp.where(is_owned, local_ids, 0), axis=0).astype(jnp.bfloat16)
        part_rows = jnp.where(is_owned[:, :, None], owned_rows, jnp.zeros((), jnp.bfloat16))
        x_rows = lax.psum_scatter(part_rows, AXIS_NAME, scatter_dimension=0, tiled=True).astype(jnp.float32)
        gain_full = lax.all_gather(gain_shard, AXIS_NAME, axis=0, tiled=True)
        wq_full = lax.all_gather(wq_shard.astype(jnp.bfloat16), AXIS_NAME, axis=0, tiled=True)
        wk_full = lax.all_gather(wk_shard.astype(jnp.bfloat16), AXIS_NAME, axis=0, tiled=True)
        wv_full = lax.all_gather(wv_shard.astype(jnp.bfloat16), AXIS_NAME, axis=0, tiled=True)
        inv_rms, h_rows, normed = norm_forward(x_rows, gain_full)
        query_proj = jnp.einsum("bsd,df->bsf", normed, wq_full, preferred_element_type=jnp.float32).astype(jnp.bfloat16)
        key_proj = jnp.einsum("bsd,df->bsf", normed, wk_full, preferred_element_type=jnp.float32).astype(jnp.bfloat16)
        value_proj = jnp.einsum("bsd,df->bsf", normed, wv_full, preferred_element_type=jnp.float32).astype(jnp.bfloat16)
        d_w_query = lax.psum_scatter(jnp.einsum("bsd,bsf->df", normed, d_query, preferred_element_type=jnp.float32), AXIS_NAME, scatter_dimension=0, tiled=True)
        d_w_key = lax.psum_scatter(jnp.einsum("bsd,bsf->df", normed, d_key, preferred_element_type=jnp.float32), AXIS_NAME, scatter_dimension=0, tiled=True)
        d_w_value = lax.psum_scatter(jnp.einsum("bsd,bsf->df", normed, d_value, preferred_element_type=jnp.float32), AXIS_NAME, scatter_dimension=0, tiled=True)
        d_normed = (jnp.einsum("bsf,df->bsd", d_query, wq_full, preferred_element_type=jnp.float32)
                    + jnp.einsum("bsf,df->bsd", d_key, wk_full, preferred_element_type=jnp.float32)
                    + jnp.einsum("bsf,df->bsd", d_value, wv_full, preferred_element_type=jnp.float32))
        d_norm_gain = lax.psum_scatter(jnp.sum(d_normed * h_rows, axis=(0, 1)), AXIS_NAME, scatter_dimension=0, tiled=True)
        u_rows = d_normed * gain_full
        d_x = inv_rms * (u_rows - h_rows * jnp.mean(u_rows * h_rows, axis=-1, keepdims=True))
        all_dx = lax.all_gather(d_x, AXIS_NAME, axis=0, tiled=True)
        scatter_ids = jnp.where(is_owned, local_ids, vocab_local)
        d_embed = jnp.zeros(embed_shard.shape, jnp.float32).at[scatter_ids].add(all_dx, mode="drop")
        return (query_proj, key_proj, value_proj, d_embed, d_norm_gain, d_w_query, d_w_key, d_w_value)

    row_spec = P(AXIS_NAME, None)
    act_spec = P(AXIS_NAME, None, None)
    vec_spec = P(AXIS_NAME)
    return jax.shard_map(local_step, mesh=mesh,
                         in_specs=(row_spec, row_spec, vec_spec, row_spec, row_spec, row_spec, act_spec, act_spec, act_spec),
                         out_specs=(act_spec, act_spec, act_spec, row_spec, vec_spec, row_spec, row_spec, row_spec),
                         check_vma=False)
```

profile of v0, /device:TPU:0, one launch (start us, length us, event | category | flops | bytes accessed | tf_op | source)
XLA Modules:
  0.0 402.2 jit_solution(3872356359847544038)
XLA Ops:
  7.2 1.6 convert_element_type.39
  8.9 0.0 reduce-scatter.14.cloned.1.call-start
  8.9 14.6 %all-gather = s32[16,1,256]{2,1,0:T(1,128)S(1)} all-gather(s32[1,1,256]{2,1,0:T(1,128)} %bitcast.82), channel_id=1, replica_groups=mesh['fsdp'=16] {'fsdp'}, dimensions={0}, use_global_device_ids=true | all-gather | bytes 17408 | tf_op jit(solution)/shard_map/all_gather | solution.py:19
  23.5 30.4 %gather_fusion = bf16[4096,896]{1,0:T(8,128)(2,1)} fusion(f32[9496,896]{1,0:T(8,128)} %param.10, s32[4096]{0:T(1024)S(1)} %broadcast_clamp_fusion), kind=kCustom, calls=%fused_computation | custom fusion | bytes 14696448 | tf_op jit(solution)/shard_map/jit(_take)/gather | solution.py:22
  54.0 7.3 %fusion.2 = bf16[16,256,896]{2,1,0:T(8,128)(2,1)} fusion(bf16[16,256,896]{2,1,0:T(8,128)(2,1)} %bitcast.76, pred[16,256]{1,0:T(8,128)(4,1)S(1)} %get-tuple-element.13, pred[16,256]{1,0:T(8,128)(4,1)S(1)} %get-tuple-element.12), kind=kLoop, calls=%fused_computation.5 | loop fusion | flops 7340032 | bytes 14688256 | tf_op jit(solution)/shard_map/jit(_where)/select_n | solution.py:23
  61.4 0.6 copy-done.5
  62.1 0.2 dynamic-update-slice
  62.3 32.4 %all-reduce = f32[896]{0:T(1024)S(1)} all-reduce(f32[896]{0:T(1024)S(1)} %dynamic-update-slice), channel_id=1, replica_groups=mesh['fsdp'=16] {'fsdp'}, use_global_device_ids=true, to_apply=%add | all-reduce | flops 896 | bytes 7168
  94.7 13.8 %all_gather.22 = bf16[896,128]{1,0:T(8,128)(2,1)S(1)} all-gather(bf16[56,128]{1,0:T(8,128)(2,1)S(1)} %convert_element_type.45), channel_id=1, replica_groups=mesh['fsdp'=16] {'fsdp'}, dimensions={0}, use_global_device_ids=true | all-gather | bytes 243712 | tf_op jit(solution)/shard_map/all_gather | solution.py:28
  108.5 12.8 %all_gather.21 = bf16[896,128]{1,0:T(8,128)(2,1)S(1)} all-gather(bf16[56,128]{1,0:T(8,128)(2,1)S(1)} %convert_element_type.42), channel_id=1, replica_groups=mesh['fsdp'=16] {'fsdp'}, dimensions={0}, use_global_device_ids=true | all-gather | bytes 243712 | tf_op jit(solution)/shard_map/all_gather | solution.py:27
  121.3 2.2 fusion.19
  123.5 0.3 convolution_add_fusion.1
  123.8 23.1 %reduce-scatter.14.cloned.1.call-done = bf16[1,256,896]{2,1,0:T(8,128)(2,1)} async-done(((bf16[16,256,896]{2,1,0:T(8,128)(2,1)}), bf16[1,256,896]{2,1,0:T(8,128)(2,1)}) %reduce-scatter.14.cloned.1.call-update) | async-done | bytes 458768 | tf_op jit(solution)/shard_map/reduce_scatter | solution.py:24
  146.8 1.3 fusion.15
  148.1 1.5 fusion.14
  149.6 2.3 fusion.13
  151.9 0.0 reduce-scatter.18.cloned.1.call-start
  152.0 2.2 fusion.24
  154.2 0.0 reduce-scatter.20.cloned.1.call-start
  154.3 1.2 fusion.21
  155.5 0.0 reduce-scatter.16.cloned.1.call-start
  155.5 2.4 fusion.17
  158.0 31.8 %all-reduce.1 = f32[896]{0:T(1024)S(1)} all-reduce(f32[896]{0:T(1024)S(1)} %get-tuple-element.8), channel_id=3, replica_groups=mesh['fsdp'=16] {'fsdp'}, use_global_device_ids=true, to_apply=%region_5.6.clone | all-reduce | flops 896 | bytes 7168
  189.8 0.6 dynamic-slice
  190.4 1.0 fusion.8
  191.3 1.0 fusion.9
  192.3 1.5 fusion.3
  193.8 26.7 %all-gather.6.cloned.1.call-done = f32[16,256,896]{2,1,0:T(8,128)} async-done(((f32[1,256,896]{2,1,0:T(8,128)}), f32[16,256,896]{2,1,0:T(8,128)}) %all-gather.6.cloned.1.call-update) | async-done | bytes 14680080 | tf_op jit(solution)/shard_map/all_gather | solution.py:42
  220.5 50.2 %scatter_custom_fusion = f32[9496,896]{1,0:T(8,128)} fusion(s32[4096]{0:T(1024)S(1)} %bitcast.81, f32[4096,896]{1,0:T(8,128)} %bitcast.83, f32[]{:T(128)} %constant.15.clone.1), kind=kCustom, calls=%fused_computation.2 | custom fusion | flops 3670016 | bytes 34034176 | tf_op jit(solution)/shard_map/scatter-add | solution.py:44
  270.7 7.0 %reduce-scatter.18.cloned.1.call-done = f32[56,128]{1,0:T(8,128)} async-done(((f32[896,128]{1,0:T(8,128)}), f32[56,128]{1,0:T(8,128)}) %reduce-scatter.18.cloned.1.call-update) | async-done | bytes 28688
  277.7 55.3 %reduce-scatter.20.cloned.1.call-done = f32[56,128]{1,0:T(8,128)} async-done(((f32[896,128]{1,0:T(8,128)}), f32[56,128]{1,0:T(8,128)}) %reduce-scatter.20.cloned.1.call-update) | async-done | bytes 28688
  333.0 62.4 %reduce-scatter.16.cloned.1.call-done = f32[56,896]{1,0:T(8,128)} async-done(((f32[896,896]{1,0:T(8,128)}), f32[56,896]{1,0:T(8,128)}) %reduce-scatter.16.cloned.1.call-update) | async-done | bytes 200720
  (35 shorter events, 0.3 us)
Async XLA Ops:
  7.2 114.1 %copy-start = (bf16[1,256,896]{2,1,0:T(8,128)(2,1)S(1)}, bf16[1,256,896]{2,1,0:T(8,128)(2,1)}, u32[]{:S(2)}) copy-start(bf16[1,256,896]{2,1,0:T(8,128)(2,1)} %param.15) | copy-start | bytes 1376260
  7.2 114.1 %all-gather.4.cloned.1.call-start = ((), (), s32[]{:S(2)}) async-start(), calls=%async_computation.5 | async-start | bytes 1705984 | tf_op jit(solution)/shard_map/all_gather | solution.py:26
  8.9 137.9 %reduce-scatter.14.cloned.1.call-start = ((), (), s32[]{:S(2)}) async-start(), calls=%async_computation.4 | async-start | bytes 7798784 | tf_op jit(solution)/shard_map/reduce_scatter | solution.py:24
  61.3 0.7 copy-start.5
  61.3 0.8 copy-start.6
  61.3 0.8 copy-start.7
  61.3 62.2 %copy-start.3 = (bf16[1,256,128]{2,1,0:T(8,128)(2,1)S(1)}, bf16[1,256,128]{2,1,0:T(8,128)(2,1)}, u32[]{:S(2)}) copy-start(bf16[1,256,128]{2,1,0:T(8,128)(2,1)} %param.16) | copy-start | bytes 196612
  61.3 86.8 %copy-start.4 = (bf16[1,256,128]{2,1,0:T(8,128)(2,1)S(1)}, bf16[1,256,128]{2,1,0:T(8,128)(2,1)}, u32[]{:S(2)}) copy-start(bf16[1,256,128]{2,1,0:T(8,128)(2,1)} %param.17) | copy-start | bytes 196612
  61.3 159.2 %all-gather.6.cloned.1.call-start = ((), (), s32[]{:S(2)}) async-start(), calls=%async_computation.6 | async-start | bytes 15597568 | tf_op jit(solution)/shard_map/all_gather | solution.py:42
  146.8 7.5 %copy-start.1 = (bf16[1,256,896]{2,1,0:T(8,128)(2,1)S(1)}, bf16[1,256,896]{2,1,0:T(8,128)(2,1)}, u32[]{:S(2)}) copy-start(bf16[1,256,896]{2,1,0:T(8,128)(2,1)} %reduce-scatter.14.cloned.1.call-done) | copy-start | bytes 1376260
  149.6 42.7 %copy-start.2 = (bf16[896,896]{1,0:T(8,128)(2,1)S(1)}, bf16[896,896]{1,0:T(8,128)(2,1)}, u32[]{:S(2)}) copy-start(bf16[896,896]{1,0:T(8,128)(2,1)} %all-gather.4.cloned.1.call-done) | copy-start | bytes 4816900
  151.9 125.8 %reduce-scatter.18.cloned.1.call-start = ((), (), s32[]{:S(2)}) async-start(), calls=%async_computation.8 | async-start | bytes 487424
  154.2 178.8 %reduce-scatter.20.cloned.1.call-start = ((), (), s32[]{:S(2)}) async-start(), calls=%async_computation.9 | async-start | bytes 487424
  155.5 239.9 %reduce-scatter.16.cloned.1.call-start = ((), (), s32[]{:S(2)}) async-start(), calls=%async_computation.7 | async-start | bytes 3411968
Sparse Core Ops, SparseCore 0:
  10.8 29.7 all-gather.3
  61.4 85.3 reduce-scatter.13
  152.0 68.4 all-gather.5
  223.2 54.5 reduce-scatter.17
  280.4 52.5 reduce-scatter.19
  335.7 59.6 reduce-scatter.15
where the time goes:
time: 403 us; the launch traced here: 402 us
  waiting for transfers between devices  175 us (43%)
  blocking collectives  105 us (26%)
  other arithmetic  62.7 us (16%)
  local copies, waits for them, and re-layouts  32 us (8%)
  between operations  14.3 us (4%)
  matrix products  13.2 us (3%)
    unnamed x9, waiting for transfers between devices  125 us
    unnamed x2, blocking collectives  64.2 us
    scatter-add x1, other arithmetic, local_step(): jnp.zeros(embed_shard.shape, jnp.float32).at[scatter_ids]  50.2 us
    gather x1, local copies, waits for them, and re-layouts, local_step(): jnp.take(embed_shard, jnp.where(is_owned, local_ids, 0), axis=0)  30.4 us
    all_gather x1, waiting for transfers between devices, local_step(): all_dx = lax.all_gather(d_x, AXIS_NAME, axis=0, tiled=True)  26.7 us
    reduce_scatter x1, waiting for transfers between devices, local_step(): lax.psum_scatter(part_rows, AXIS_NAME, scatter_dimension=0, tiled=True)  23.1 us
    all_gather x1, blocking collectives, local_step(): all_tokens = lax.all_gather(tokens, AXIS_NAME, axis=0, tiled=True)  14.6 us
    all_gather x1, blocking collectives, local_step(): lax.all_gather(wv_shard.astype(jnp.bfloat16), AXIS_NAME, axis=0, tiled=True)  13.8 us
  transfers between devices with their start and end apart: 6, of which 5 were waited for; matrix products, arithmetic and copies ran while one was open for 25% of the time, Pallas kernels for 0%

commit v1 on v0

v1 whole, which is shorter than its diff:
```python
import functools
import jax
import jax.numpy as jnp
from jax import lax
from jax.experimental import pallas as pl
from jax.experimental.pallas import tpu as pltpu
from jax.sharding import PartitionSpec as P

AXIS_NAME = "fsdp"
NDEV = 16
STRIDES = (2, 4, 8)
MESH = pl.DeviceIdType.MESH
SEQ = 256
DM = 896
DF = 1152
WROWS = 56
F32 = jnp.float32
BF16 = jnp.bfloat16


def flip(me, stride):
    return me + stride * (1 - 2 * ((me // stride) % 2))


def flip_mask(me, mask, order=(0, 1, 2)):
    for pos in range(3):
        if (mask >> pos) & 1:
            me = flip(me, STRIDES[order[pos]])
    return me


def colour_order(c):
    return (c, (c + 1) % 3, (c + 2) % 3)


def remote(src, dst, send, recv, dev):
    return pltpu.make_async_remote_copy(src_ref=src, dst_ref=dst, send_sem=send, recv_sem=recv,
                                        device_id=(dev,), device_id_type=MESH)


def barrier_all(me):
    sem = pltpu.get_barrier_semaphore()
    for k in range(1, NDEV):
        pl.semaphore_signal(sem, inc=1, device_id=((me + k) % NDEV,), device_id_type=MESH)
    pl.semaphore_wait(sem, NDEV - 1)


class Gather:
    def __init__(self, me, src, dst, sems, width):
        self.me, self.src, self.dst, self.width = me, src, dst, width
        self.send, self.recv, self.csend, self.crecv = sems

    def cols(self, c):
        return pl.ds(c * self.width, self.width)

    def block(self, c, mask, base=None):
        origin = flip_mask(self.me if base is None else base, mask, colour_order(c))
        return self.dst.at[origin, :, self.cols(c)]

    def link_copy(self, c, mask, pos):
        src = self.src.at[:, self.cols(c)] if mask == 0 else self.block(c, mask)
        new = mask | (1 << pos)
        return remote(src, self.block(c, mask), self.send.at[c, new], self.recv.at[c, new],
                      flip(self.me, STRIDES[colour_order(c)[pos]]))

    def core_copy(self, c, mask):
        src = self.src.at[:, self.cols(c)] if mask == 0 else self.block(c, mask)
        return remote(src, self.block(c, mask), self.csend.at[c, mask], self.crecv.at[c, mask], flip(self.me, 1))

    def start_piece(self, c, mask):
        for pos in range(mask.bit_length(), 3):
            self.link_copy(c, mask, pos).start()
        self.core_copy(c, mask).start()

    def wait_piece(self, c, mask):
        pos = mask.bit_length() - 1
        self.link_copy(c, mask & ~(1 << pos), pos).wait_recv()

    def finish(self):
        for c in range(3):
            for mask in range(8):
                for pos in range(mask.bit_length(), 3):
                    self.link_copy(c, mask, pos).wait_send()
                self.core_copy(c, mask).wait()


def gather_kernel(tok, gain, w, d, tok_o, gain_o, w_o, d_o, small_send, small_recv, loc,
                  ws, wr, wcs, wcr, ds, dr, dcs, dcr):
    me = lax.axis_index(AXIS_NAME)
    own = [pltpu.make_async_copy(tok, tok_o.at[me], loc.at[0]), pltpu.make_async_copy(gain, gain_o.at[me], loc.at[1]),
           pltpu.make_async_copy(w, w_o.at[me], loc.at[2]), pltpu.make_async_copy(d, d_o.at[me], loc.at[3])]
    for copy in own:
        copy.start()
    barrier_all(me)
    small = []
    for k in range(1, NDEV):
        dev = (me + k) % NDEV
        small.append(remote(tok, tok_o.at[me], small_send.at[0, k], small_recv.at[0, k], dev))
        small.append(remote(gain, gain_o.at[me], small_send.at[1, k], small_recv.at[1, k], dev))
    for copy in small:
        copy.start()
    wg = Gather(me, w, w_o, (ws, wr, wcs, wcr), DF // 3)
    dg = Gather(me, d, d_o, (ds, dr, dcs, dcr), DF // 3)
    for g in (wg, dg):
        for c in range(3):
            g.start_piece(c, 0)
    for mask in range(1, 8):
        for g in (wg, dg):
            for c in range(3):
                g.wait_piece(c, mask)
                g.start_piece(c, mask)
    wg.finish()
    dg.finish()
    for copy in small:
        copy.wait()
    for copy in own:
        copy.wait()


def gather_all(tok, gain, w, d):
    vm = pl.BlockSpec(memory_space=pltpu.VMEM)
    hbm = pl.BlockSpec(memory_space=pl.ANY)
    dma = pltpu.SemaphoreType.DMA
    return pl.pallas_call(
        gather_kernel,
        out_shape=(jax.ShapeDtypeStruct((NDEV, 1, SEQ), jnp.int32), jax.ShapeDtypeStruct((NDEV, 1, 128), F32),
                   jax.ShapeDtypeStruct((NDEV, WROWS, DF), BF16), jax.ShapeDtypeStruct((NDEV, SEQ, DF), BF16)),
        in_specs=[vm] * 4,
        out_specs=(hbm,) * 4,
        scratch_shapes=[dma((2, NDEV)), dma((2, NDEV)), dma((4,))] + [dma((3, 8))] * 8,
        compiler_params=pltpu.CompilerParams(collective_id=0, has_side_effects=True),
        name="gather_all",
    )(tok, gain, w, d)


class Scatter:
    def __init__(self, me, part, acc, bufs, sems, piece):
        self.me, self.part, self.acc, self.piece = me, part, acc, piece
        self.r0, self.r = bufs[0], bufs[1:]
        self.csend, self.crecv, self.send, self.recv = sems

    def core_copy(self, mask):
        block = flip_mask(flip(self.me, 1), mask)
        return remote(self.part(block), self.r0.at[mask], self.csend.at[mask], self.crecv.at[mask], flip(self.me, 1))

    def phase_copy(self, c, phase, rel):
        order = colour_order(c)
        absmask = sum(1 << order[pos] for pos in range(3) if (rel >> pos) & 1)
        low = rel >> (phase + 1)
        sem = (0, 4, 6)[phase] + low
        return remote(self.piece(self.acc.at[absmask], c), self.piece(self.r[phase].at[low], c),
                      self.send.at[c, sem], self.recv.at[c, sem], flip(self.me, STRIDES[order[phase]]))

    def core_start(self):
        for mask in (7, 3, 6, 5, 1, 2, 4, 0):
            self.core_copy(mask).start()

    def core_done(self, mask):
        self.core_copy(mask).wait_recv()
        self.acc[mask] = self.part(flip_mask(self.me, mask))[...] + self.r0[mask]
        for c in range(3):
            if (mask >> c) & 1:
                order = colour_order(c)
                rel = sum(1 << pos for pos in range(3) if (mask >> order[pos]) & 1)
                self.phase_copy(c, 0, rel).start()

    def phase_done(self, c, phase, low):
        order = colour_order(c)
        rel = low << (phase + 1)
        self.phase_copy(c, phase, rel | (1 << phase)).wait_recv()
        absmask = sum(1 << order[pos] for pos in range(3) if (rel >> pos) & 1)
        dst = self.piece(self.acc.at[absmask], c)
        dst[...] = dst[...] + self.piece(self.r[phase].at[low], c)[...]

    def move_on(self, c, phase, rel):
        self.phase_copy(c, phase, rel).start()

    def steps(self):
        out = [functools.partial(self.core_done, mask) for mask in (7, 3, 6, 5, 1, 2, 4, 0)]

        def phase0(c, low):
            self.phase_done(c, 0, low)
            if low & 1:
                self.move_on(c, 1, low << 1)

        def phase1(c, low):
            self.phase_done(c, 1, low)
            if low & 1:
                self.move_on(c, 2, low << 2)

        for low in (3, 1, 2, 0):
            out += [functools.partial(phase0, c, low) for c in range(3)]
        for low in (1, 0):
            out += [functools.partial(phase1, c, low) for c in range(3)]
        out += [functools.partial(self.phase_done, c, 2, 0) for c in range(3)]
        return out

    def finish(self):
        for mask in range(8):
            self.core_copy(mask).wait_send()
        for c in range(3):
            for phase in range(3):
                for low in range(4 >> phase):
                    self.phase_copy(c, phase, (low << (phase + 1)) | (1 << phase)).wait_send()


ROW_PIECES = ((0, 96), (96, 80), (176, 80))


def row_piece(ref, c):
    start, size = ROW_PIECES[c]
    return ref.at[pl.ds(start, size)]


def col_piece(ref, c):
    return ref.at[:, pl.ds(c * (DF // 3), DF // 3)]


def step_kernel(xp, g, w, gain, d, qkv_o, dx_o, dw_o, dg_o,
                gbuf, gsem, dxbuf, dxsem, xacc, x0, x1, x2, x3, xcs, xcr, xs, xr,
                dwp, wacc, w0, w1, w2, w3, wcs, wcr, ws, wr, dgp, dgsum, dgall, dgs, dgr):
    me = lax.axis_index(AXIS_NAME)
    load = lambda b, slot: pltpu.make_async_copy(g.at[b], gbuf.at[slot], gsem.at[slot])
    load(0, 0).start()
    dgall[...] = jnp.zeros_like(dgall)
    barrier_all(me)
    xrs = Scatter(me, lambda b: xp.at[b], xacc, (x0, x1, x2, x3), (xcs, xcr, xs, xr), row_piece)
    xrs.core_start()
    events = xrs.steps()
    dgp[...] = jnp.zeros_like(dgp)
    store = lambda b, slot: pltpu.make_async_copy(dxbuf.at[slot], dx_o.at[b], dxsem.at[slot])
    per = -(-len(events) // NDEV)

    @pl.loop(0, NDEV)
    def _(b):
        slot = b % 2

        @pl.when(b + 1 < NDEV)
        def _():
            load(b + 1, 1 - slot).start()

        load(b, slot).wait()

        @pl.when(b >= 2)
        def _():
            store(b - 2, slot).wait()

        dn = lax.dot_general(gbuf[slot], w[...], (((1,), (1,)), ((), ())), preferred_element_type=F32)
        x = xp[b].astype(F32)
        r = lax.rsqrt(jnp.mean(x * x, axis=-1, keepdims=True) + 1e-5)
        h = x * r
        dgp[...] += jnp.sum((dn * h).reshape(SEQ // 8, 8, DM), axis=0)
        u = dn * gain[...]
        dxbuf[slot] = r * (u - h * jnp.mean(u * h, axis=-1, keepdims=True))
        store(b, slot).start()
        for k in range(NDEV):
            group = events[k * per:(k + 1) * per]
            if group:
                @pl.when(b == k)
                def _(group=group):
                    for event in group:
                        event()

    dgsum[...] = jnp.broadcast_to(jnp.sum(dgp[...], axis=0, keepdims=True), dgsum.shape)
    dgall[me] = dgsum[...]
    small = [remote(dgsum.at[pl.ds(0, 1)], dgall.at[me, pl.ds(0, 1)], dgs.at[k], dgr.at[k], (me + k) % NDEV) for k in range(1, NDEV)]
    for copy in small:
        copy.start()
    x = xacc[0].astype(F32)
    r = lax.rsqrt(jnp.mean(x * x, axis=-1, keepdims=True) + 1e-5)
    n = (x * r * gain[...]).astype(BF16)
    dwp[...] = lax.dot_general(n, d[...], (((0,), (0,)), ((), ())), preferred_element_type=F32)
    part = lambda b: dwp.at[pl.ds(pl.multiple_of(b * WROWS, 8), WROWS)]
    wrs = Scatter(me, part, wacc, (w0, w1, w2, w3), (wcs, wcr, ws, wr), col_piece)
    wrs.core_start()
    qkv_o[...] = jnp.dot(n, w[...], preferred_element_type=F32).astype(BF16)
    for event in wrs.steps():
        event()
    dw_o[...] = wacc[0]
    for copy in small:
        copy.wait()
    dg_o[...] = jnp.sum(dgall[...], axis=0)
    store(NDEV - 2, 0).wait()
    store(NDEV - 1, 1).wait()
    xrs.finish()
    wrs.finish()


def step_all(xp, g, w, gain, d):
    vm = pl.BlockSpec(memory_space=pltpu.VMEM)
    hbm = pl.BlockSpec(memory_space=pl.ANY)
    dma = pltpu.SemaphoreType.DMA
    vmem = pltpu.VMEM
    xb = lambda k: vmem((k, SEQ, DM), BF16)
    wb = lambda k: vmem((k, WROWS, DF), F32)
    return pl.pallas_call(
        step_kernel,
        out_shape=(jax.ShapeDtypeStruct((SEQ, DF), BF16), jax.ShapeDtypeStruct((NDEV, SEQ, DM), F32),
                   jax.ShapeDtypeStruct((WROWS, DF), F32), jax.ShapeDtypeStruct((8, DM), F32)),
        in_specs=[vm, hbm, vm, vm, vm],
        out_specs=(vm, hbm, vm, vm),
        scratch_shapes=[vmem((2, SEQ, DF), BF16), dma((2,)), vmem((2, SEQ, DM), F32), dma((2,)),
                        xb(8), xb(8), xb(4), xb(2), xb(1), dma((8,)), dma((8,)), dma((3, 7)), dma((3, 7)),
                        vmem((DM, DF), F32), wb(8), wb(8), wb(4), wb(2), wb(1),
                        dma((8,)), dma((8,)), dma((3, 7)), dma((3, 7)),
                        vmem((8, DM), F32), vmem((8, DM), F32), vmem((NDEV, 8, DM), F32), dma((NDEV,)), dma((NDEV,))],
        compiler_params=pltpu.CompilerParams(collective_id=1, has_side_effects=True, vmem_limit_bytes=62 * 2**20),
        name="step_all",
    )(xp, g, w, gain, d)


def solution(mesh):
    def local_step(tokens, embed_shard, gain_shard, wq_shard, wk_shard, wv_shard, d_query, d_key, d_value):
        vocab_local = embed_shard.shape[0]
        dev_index = lax.axis_index(AXIS_NAME)
        w_shard = jnp.concatenate([wq_shard, wk_shard, wv_shard], axis=1).astype(BF16)
        d_own = jnp.concatenate([d_query[0], d_key[0], d_value[0]], axis=1)
        gain_pad = jnp.pad(gain_shard[None], ((0, 0), (0, 128 - WROWS)))
        tok_all, gain_all, w_all, d_all = gather_all(tokens, gain_pad, w_shard, d_own)
        gain_full = gain_all[:, 0, :WROWS].reshape(1, DM)
        w_full = w_all.reshape(DM, DF)
        local_ids = tok_all[:, 0, :] - dev_index * vocab_local
        is_owned = (local_ids >= 0) & (local_ids < vocab_local)
        owned_rows = jnp.take(embed_shard, jnp.where(is_owned, local_ids, 0), axis=0).astype(BF16)
        part_rows = jnp.where(is_owned[:, :, None], owned_rows, jnp.zeros((), BF16))
        qkv, dx_all, dw, dgain = step_all(part_rows, d_all, w_full, gain_full, d_own)
        scatter_ids = jnp.where(is_owned, local_ids, vocab_local)
        d_embed = jnp.zeros(embed_shard.shape, F32).at[scatter_ids].add(dx_all, mode="drop")
        d_norm_gain = lax.dynamic_slice(dgain, (0, dev_index * WROWS), (1, WROWS))[0]
        return (qkv[None, :, :DM], qkv[None, :, DM:DM + 128], qkv[None, :, DM + 128:], d_embed, d_norm_gain,
                dw[:, :DM], dw[:, DM:DM + 128], dw[:, DM + 128:])

    row_spec = P(AXIS_NAME, None)
    act_spec = P(AXIS_NAME, None, None)
    vec_spec = P(AXIS_NAME)
    return jax.shard_map(local_step, mesh=mesh,
                         in_specs=(row_spec, row_spec, vec_spec, row_spec, row_spec, row_spec, act_spec, act_spec, act_spec),
                         out_specs=(act_spec, act_spec, act_spec, row_spec, vec_spec, row_spec, row_spec, row_spec),
                         check_vma=False)
```

time: 403 us -> 210 us (0.52)
  waiting for transfers between devices: 175 us -> 0 us
  Pallas kernels: 0 us -> 105 us
  blocking collectives: 105 us -> 0 us
  between operations: 14.3 us -> 0.69 us
  matrix products: 13.2 us -> 0 us
  local copies, waits for them, and re-layouts: 32 us -> 40.6 us
    unnamed x9 -> x0, waiting for transfers between devices: 125 us -> none
    pallas_call x0 -> x2, Pallas kernels: none -> 105 us  [the longest x1 56.3 us: step_all(): pl.pallas_call(step_kernel, out_shape=(jax.ShapeDtypeStruct((SEQ, DF), BF...]
    unnamed x2 -> x0, blocking collectives: 64.2 us -> none
    all_gather x3 -> x0, blocking collectives: 41.2 us -> none  [the longest x1 14.6 us: local_step(): all_tokens = lax.all_gather(tokens, AXIS_NAME, axis=0, tiled=True)]
    all_gather x2 -> x0, waiting for transfers between devices: 26.7 us -> none  [the longest x1 26.7 us: local_step(): all_dx = lax.all_gather(d_x, AXIS_NAME, axis=0, tiled=True)]
    reduce_scatter x1 -> x0, waiting for transfers between devices: 23.1 us -> none  [local_step(): lax.psum_scatter(part_rows, AXIS_NAME, scatter_dimension=0, tiled=True)]
    dot_general x9 -> x0, matrix products: 13.2 us -> none  [the longest x1 2.41 us: local_step(): jnp.einsum('bsd,bsf->df', normed, d_query, preferred_element_type=jnp.flo...]
    select_n x1 -> x3, other arithmetic: 7.29 us -> 8.06 us  [the longest x1 7.27 us: local_step(): part_rows = jnp.where(is_owned[:, :, None], owned_rows, jnp.zeros((), BF16))]
  transfers between devices with their start and end apart: 6 -> 0, of which waited for: 5 -> 0; matrix products, arithmetic and copies ran while one was open for 25% -> 0% of each run, Pallas kernels for 0% -> 0%
where the time goes in v1:
time: 210 us; the launch traced here: 209 us
  Pallas kernels  105 us (50%)
  other arithmetic  63.3 us (30%)
  local copies, waits for them, and re-layouts  40.6 us (19%)
    pallas_call x1, Pallas kernels, step_all(): pl.pallas_call(step_kernel, out_shape=(jax.ShapeDtypeStruct((SEQ, DF), BF...  56.3 us
    scatter-add x1, other arithmetic, local_step(): jnp.zeros(embed_shard.shape, F32).at[scatter_ids].add(dx_all, mode='drop')  50.2 us
    pallas_call x1, Pallas kernels, gather_all(): pl.pallas_call(gather_kernel, out_shape=(jax.ShapeDtypeStruct((NDEV, 1, S...  48.3 us
    gather x1, local copies, waits for them, and re-layouts, local_step(): jnp.take(embed_shard, jnp.where(is_owned, local_ids, 0), axis=0)  30.4 us
    select_n x1, other arithmetic, local_step(): part_rows = jnp.where(is_owned[:, :, None], owned_rows, jnp.zeros((), BF16))  7.27 us

profile of v1, /device:TPU:0, one launch (start us, length us, event | category | flops | bytes accessed | tf_op | source)
XLA Modules:
  0.0 209.2 jit_solution(17130910034116123386)
XLA Ops:
  0.6 1.2 pad.4.gain
  1.8 0.8 convert.10
  2.6 0.8 convert.11
  3.3 0.9 convert.9
  4.3 0.7 pad_maximum_fusion.1.w
  4.9 2.0 pad_maximum_fusion.d
  6.9 48.3 %gather_all.1 = (s32[16,1,256]{2,1,0:T(1,128)}, f32[16,1,128]{2,1,0:T(1,128)}, bf16[16,56,1152]{2,1,0:T(8,128)(2,1)}, bf16[16,256,1152]{2,1,0:T(8,128)(2,1)}) custom-call(s32[1,256]{1,0:T(1,128)} %tok.1, f32[1,128]{1,0:T(1,128)} %pad.4.gain, bf16[56,1152]{1,0:T(8,128)(2,1)} %pad_maximum_fusion.1.w, bf16[256,1152]{1,0:T(8,128)(2,1)} %pad_maximum_fusion.d), custom_call_target="tpu_custom_call" | custom-call | tf_op jit(solution)/shard_map/gather_all/pallas_call | solution.py:124
  55.2 0.7 slice_reduce_fusion
  55.9 0.7 reshape_squeeze.3.gain
  56.6 0.8 compare_select_fusion
  57.4 30.4 %gather_fusion = bf16[4096,896]{1,0:T(8,128)(2,1)} fusion(f32[9496,896]{1,0:T(8,128)} %param.10, s32[4096]{0:T(1024)S(1)} %broadcast_clamp_fusion), kind=kCustom, calls=%fused_computation | custom fusion | bytes 14696448 | tf_op jit(solution)/shard_map/jit(_take)/gather | solution.py:324
  87.8 7.3 %fusion.2.xp = bf16[16,256,896]{2,1,0:T(8,128)(2,1)} fusion(bf16[16,256,896]{2,1,0:T(8,128)(2,1)} %bitcast.34, pred[16,256]{1,0:T(8,128)(4,1)S(1)} %get-tuple-element.31, pred[16,256]{1,0:T(8,128)(4,1)S(1)} %get-tuple-element.30), kind=kLoop, calls=%fused_computation.5 | loop fusion | flops 7340032 | bytes 14688256 | tf_op jit(solution)/shard_map/jit(_where)/select_n | solution.py:325
  95.1 56.3 %step_all.1 = (bf16[256,1152]{1,0:T(8,128)(2,1)}, f32[16,256,896]{2,1,0:T(8,128)}, f32[56,1152]{1,0:T(8,128)}, f32[8,896]{1,0:T(8,128)}) custom-call(bf16[16,256,896]{2,1,0:T(8,128)(2,1)} %fusion.2.xp, bf16[16,256,1152]{2,1,0:T(8,128)(2,1)} %get-tuple-element.17.g, bf16[896,1152]{1,0:T(8,128)(2,1)} %bitcast.35, f32[1,896]{1,0:T(1,128)} %reshape_squeeze.3.gain, ...), custom_call_target="tpu_custom_call" | custom-call | tf_op jit(solution)/shard_map/step_all/pallas_call | solution.py:296
  151.4 1.3 dynamic-slice_bitcast_fusion
  152.7 1.4 fusion.6
  154.1 1.6 slice.25
  155.7 1.5 slice_bitcast_fusion.1
  157.2 1.8 slice_bitcast_fusion
  159.0 50.2 %scatter_custom_fusion = f32[9496,896]{1,0:T(8,128)} fusion(s32[4096]{0:T(1024)S(1)} %bitcast.40, f32[4096,896]{1,0:T(8,128)} %bitcast.41, f32[]{:T(128)} %constant.9.clone.1), kind=kCustom, calls=%fused_computation.2 | custom fusion | flops 3670016 | bytes 34034176 | tf_op jit(solution)/shard_map/scatter-add | solution.py:328
  (3 shorter events, 0.1 us)

commit v2 on v1

--- a/solution.py
+++ b/solution.py
@@ -84,53 +84,103 @@
                 self.core_copy(c, mask).wait()
 
 
-def gather_kernel(tok, gain, w, d, tok_o, gain_o, w_o, d_o, small_send, small_recv, loc,
-                  ws, wr, wcs, wcr, ds, dr, dcs, dcr):
+def gather_kernel(tok, gain, wq, wk, wv, dq, dk, dv, table, tok_o, gain_o, w_o, d_o, xp_o,
+                  wpad, d, ids, tab, rows, xbuf, xsem, small_send, small_recv, loc, ws, wr, wcs, wcr, ds, dr, dcs, dcr):
     me = lax.axis_index(AXIS_NAME)
+    vocab = table.shape[0]
+    table_copy = pltpu.make_async_copy(table, tab.at[pl.ds(0, vocab)], loc.at[4])
+    table_copy.start()
+    for ref, src in ((wpad, (wq, wk, wv)), (d, (dq, dk, dv))):
+        height = src[0].shape[0]
+        ref[:height, :DM] = src[0][...].astype(BF16)
+        ref[:height, DM:DM + 128] = src[1][...].astype(BF16)
+        ref[:height, DM + 128:] = src[2][...].astype(BF16)
+    w = wpad.at[pl.ds(0, WROWS)]
+    tab[pl.ds(vocab, 8)] = jnp.zeros((8, DM), F32)
     own = [pltpu.make_async_copy(tok, tok_o.at[me], loc.at[0]), pltpu.make_async_copy(gain, gain_o.at[me], loc.at[1]),
            pltpu.make_async_copy(w, w_o.at[me], loc.at[2]), pltpu.make_async_copy(d, d_o.at[me], loc.at[3])]
     for copy in own:
         copy.start()
     barrier_all(me)
-    small = []
+    tok_copies, gain_copies = [], []
     for k in range(1, NDEV):
         dev = (me + k) % NDEV
-        small.append(remote(tok, tok_o.at[me], small_send.at[0, k], small_recv.at[0, k], dev))
-        small.append(remote(gain, gain_o.at[me], small_send.at[1, k], small_recv.at[1, k], dev))
-    for copy in small:
+        tok_copies.append(remote(tok, tok_o.at[me], small_send.at[0, k], small_recv.at[0, k], dev))
+        gain_copies.append(remote(gain, gain_o.at[me], small_send.at[1, k], small_recv.at[1, k], dev))
+    for copy in tok_copies + gain_copies:
         copy.start()
     wg = Gather(me, w, w_o, (ws, wr, wcs, wcr), DF // 3)
     dg = Gather(me, d, d_o, (ds, dr, dcs, dcr), DF // 3)
     for g in (wg, dg):
         for c in range(3):
             g.start_piece(c, 0)
-    for mask in range(1, 8):
-        for g in (wg, dg):
-            for c in range(3):
-                g.wait_piece(c, mask)
-                g.start_piece(c, mask)
+    for copy in tok_copies:
+        copy.wait()
+    own[0].wait()
+    ids_copy = pltpu.make_async_copy(tok_o, ids, loc.at[5])
+    ids_copy.start()
+
+    def piece(g, c, mask):
+        g.wait_piece(c, mask)
+        g.start_piece(c, mask)
+
+    events = [functools.partial(piece, g, c, mask) for mask in range(1, 8) for g in (wg, dg) for c in range(3)]
+    ids_copy.wait()
+    table_copy.wait()
+    per = -(-len(events) // NDEV)
+    store = lambda b, slot: pltpu.make_async_copy(xbuf.at[slot], xp_o.at[b], xsem.at[slot])
+
+    @pl.loop(0, NDEV)
+    def _(b):
+        slot = b % 2
+
+        @pl.loop(0, SEQ // 8)
+        def _(i):
+            for j in range(8):
+                local = ids[b, 0, i * 8 + j] - me * vocab
+                owned = (local >= 0) & (local < vocab)
+                rows[pl.ds(i * 8 + j, 1), :] = tab[pl.ds(jnp.where(owned, local, vocab), 1), :]
+
+        @pl.when(b >= 2)
+        def _():
+            store(b - 2, slot).wait()
+
+        xbuf[slot] = rows[0:SEQ].astype(BF16)
+        store(b, slot).start()
+        for k in range(NDEV):
+            group = events[k * per:(k + 1) * per]
+            if group:
+                @pl.when(b == k)
+                def _(group=group):
+                    for event in group:
+                        event()
+
+    store(NDEV - 2, 0).wait()
+    store(NDEV - 1, 1).wait()
     wg.finish()
     dg.finish()
-    for copy in small:
+    for copy in gain_copies + own[1:]:
         copy.wait()
-    for copy in own:
-        copy.wait()
-
-
-def gather_all(tok, gain, w, d):
+
+
+def gather_all(tok, gain, weights, grads, table):
     vm = pl.BlockSpec(memory_space=pltpu.VMEM)
     hbm = pl.BlockSpec(memory_space=pl.ANY)
     dma = pltpu.SemaphoreType.DMA
+    vmem = pltpu.VMEM
     return pl.pallas_call(
         gather_kernel,
-        out_shape=(jax.ShapeDtypeStruct((NDEV, 1, SEQ), jnp.int32), jax.ShapeDtypeStruct((NDEV, 1, 128), F32),
-                   jax.ShapeDtypeStruct((NDEV, WROWS, DF), BF16), jax.ShapeDtypeStruct((NDEV, SEQ, DF), BF16)),
-        in_specs=[vm] * 4,
-        out_specs=(hbm,) * 4,
-        scratch_shapes=[dma((2, NDEV)), dma((2, NDEV)), dma((4,))] + [dma((3, 8))] * 8,
-        compiler_params=pltpu.CompilerParams(collective_id=0, has_side_effects=True),
+        out_shape=(jax.ShapeDtypeStruct((NDEV, 1, SEQ), jnp.int32), jax.ShapeDtypeStruct((NDEV, 1, WROWS), F32),
+                   jax.ShapeDtypeStruct((NDEV, WROWS, DF), BF16), jax.ShapeDtypeStruct((NDEV, SEQ, DF), BF16),
+                   jax.ShapeDtypeStruct((NDEV, SEQ, DM), BF16)),
+        in_specs=[vm] * 8 + [hbm],
+        out_specs=(hbm,) * 5,
+        scratch_shapes=[vmem((64, DF), BF16), vmem((SEQ, DF), BF16), pltpu.SMEM((NDEV, 1, SEQ), jnp.int32),
+                        vmem((table.shape[0] + 16, DM), F32), vmem((SEQ + 8, DM), F32), vmem((2, SEQ, DM), BF16), dma((2,)),
+                        dma((2, NDEV)), dma((2, NDEV)), dma((6,))] + [dma((3, 8))] * 8,
+        compiler_params=pltpu.CompilerParams(collective_id=0, has_side_effects=True, vmem_limit_bytes=56 * 2**20),
         name="gather_all",
-    )(tok, gain, w, d)
+    )(tok, gain, *weights, *grads, table)
 
 
 class Scatter:
@@ -216,12 +266,14 @@
     return ref.at[:, pl.ds(c * (DF // 3), DF // 3)]
 
 
-def step_kernel(xp, g, w, gain, d, qkv_o, dx_o, dw_o, dg_o,
-                gbuf, gsem, dxbuf, dxsem, xacc, x0, x1, x2, x3, xcs, xcr, xs, xr,
+def step_kernel(xp, g, w, gain, qkv_o, dx_o, dw_o, dg_o,
+                d, dsem, gbuf, gsem, dxbuf, dxsem, xacc, x0, x1, x2, x3, xcs, xcr, xs, xr,
                 dwp, wacc, w0, w1, w2, w3, wcs, wcr, ws, wr, dgp, dgsum, dgall, dgs, dgr):
     me = lax.axis_index(AXIS_NAME)
     load = lambda b, slot: pltpu.make_async_copy(g.at[b], gbuf.at[slot], gsem.at[slot])
     load(0, 0).start()
+    d_copy = pltpu.make_async_copy(g.at[me], d, dsem)
+    d_copy.start()
     dgall[...] = jnp.zeros_like(dgall)
     barrier_all(me)
     xrs = Scatter(me, lambda b: xp.at[b], xacc, (x0, x1, x2, x3), (xcs, xcr, xs, xr), row_piece)
@@ -266,6 +318,7 @@
     small = [remote(dgsum.at[pl.ds(0, 1)], dgall.at[me, pl.ds(0, 1)], dgs.at[k], dgr.at[k], (me + k) % NDEV) for k in range(1, NDEV)]
     for copy in small:
         copy.start()
+    d_copy.wait()
     x = xacc[0].astype(F32)
     r = lax.rsqrt(jnp.mean(x * x, axis=-1, keepdims=True) + 1e-5)
     n = (x * r * gain[...]).astype(BF16)
@@ -286,7 +339,7 @@
     wrs.finish()
 
 
-def step_all(xp, g, w, gain, d):
+def step_all(xp, g, w, gain):
     vm = pl.BlockSpec(memory_space=pltpu.VMEM)
     hbm = pl.BlockSpec(memory_space=pl.ANY)
     dma = pltpu.SemaphoreType.DMA
@@ -297,38 +350,104 @@
         step_kernel,
         out_shape=(jax.ShapeDtypeStruct((SEQ, DF), BF16), jax.ShapeDtypeStruct((NDEV, SEQ, DM), F32),
                    jax.ShapeDtypeStruct((WROWS, DF), F32), jax.ShapeDtypeStruct((8, DM), F32)),
-        in_specs=[vm, hbm, vm, vm, vm],
+        in_specs=[vm, hbm, vm, vm],
         out_specs=(vm, hbm, vm, vm),
-        scratch_shapes=[vmem((2, SEQ, DF), BF16), dma((2,)), vmem((2, SEQ, DM), F32), dma((2,)),
+        scratch_shapes=[vmem((SEQ, DF), BF16), dma, vmem((2, SEQ, DF), BF16), dma((2,)), vmem((2, SEQ, DM), F32), dma((2,)),
                         xb(8), xb(8), xb(4), xb(2), xb(1), dma((8,)), dma((8,)), dma((3, 7)), dma((3, 7)),
                         vmem((DM, DF), F32), wb(8), wb(8), wb(4), wb(2), wb(1),
                         dma((8,)), dma((8,)), dma((3, 7)), dma((3, 7)),
                         vmem((8, DM), F32), vmem((8, DM), F32), vmem((NDEV, 8, DM), F32), dma((NDEV,)), dma((NDEV,))],
         compiler_params=pltpu.CompilerParams(collective_id=1, has_side_effects=True, vmem_limit_bytes=62 * 2**20),
         name="step_all",
-    )(xp, g, w, gain, d)
+    )(xp, g, w, gain)
+
+
+def embed_kernel(keys, starts, dx, qkv, dw, de_o, q_o, k_o, v_o, dwq_o, dwk_o, dwv_o, dxv, de, insem, outsem):
+    vocab = de_o.shape[0]
+    fetch = pltpu.make_async_copy(dx, dxv.at[pl.ds(0, NDEV * SEQ)], insem)
+    fetch.start()
+
+    @pl.loop(0, (vocab + 8) // 32)
+    def _(i):
+        de[pl.ds(pl.multiple_of(i * 32, 32), 32)] = jnp.zeros((32, DM), F32)
+
+    for outs, ref in (((q_o, k_o, v_o), qkv), ((dwq_o, dwk_o, dwv_o), dw)):
+        outs[0][...] = ref[:, :DM]
+        outs[1][...] = ref[:, DM:DM + 128]
+        outs[2][...] = ref[:, DM + 128:]
+    fetch.wait()
+
+    def token(pos, carry):
+        prev, total = carry
+        key = keys[pos]
+        row = lax.shift_right_logical(key, 12)
+        part = dxv[pl.ds(key & 4095, 1), :]
+        total = jnp.where(row == prev, total, 0.0) + part
+        de[pl.ds(row, 1), :] = total
+        return row, total
+
+    def group(g, carry):
+        first = (starts[0] - 1 - g) * 8
+        for j in range(7, -1, -1):
+            carry = token(first + j, carry)
+        return carry
+
+    carry = (jnp.int32(-1), jnp.zeros((1, DM), F32))
+    done = jnp.int32(0)
+    copies = []
+    bounds = embed_bounds(vocab)
+    for k in range(len(bounds) - 1):
+        upto = starts[0] - starts[k + 1]
+        carry = lax.fori_loop(done, upto, group, carry)
+        done = upto
+        low, high = bounds[k + 1], bounds[k]
+        copies.append(pltpu.make_async_copy(de.at[pl.ds(low, high - low)], de_o.at[pl.ds(low, high - low)], outsem.at[k]))
+        copies[-1].start()
+    for copy in copies:
+        copy.wait()
+
+
+def embed_bounds(vocab):
+    blocks = 16
+    return [vocab] + [(vocab * k // blocks) // 8 * 8 for k in range(blocks - 1, 0, -1)] + [0]
+
+
+def embed_all(local_ids, is_owned, dx, qkv, dw, vocab):
+    order = jnp.arange(NDEV * SEQ, dtype=jnp.int32)
+    keys = jnp.sort(jnp.where(is_owned, local_ids, vocab).reshape(-1) * 4096 + order)
+    bounds = jnp.array(embed_bounds(vocab), jnp.int32)
+    below = jnp.sum((keys[None, :] < bounds[:, None] * 4096).astype(jnp.int32), axis=1)
+    starts = jnp.concatenate([(below[:1] + 7) // 8, below[1:] // 8])
+    vm = pl.BlockSpec(memory_space=pltpu.VMEM)
+    hbm = pl.BlockSpec(memory_space=pl.ANY)
+    smem = pl.BlockSpec(memory_space=pltpu.SMEM)
+    sds = jax.ShapeDtypeStruct
+    return pl.pallas_call(
+        embed_kernel,
+        out_shape=(sds((vocab, DM), F32), sds((SEQ, DM), BF16), sds((SEQ, 128), BF16), sds((SEQ, 128), BF16),
+                   sds((WROWS, DM), F32), sds((WROWS, 128), F32), sds((WROWS, 128), F32)),
+        in_specs=[smem, smem, hbm, vm, vm],
+        out_specs=(hbm,) + (vm,) * 6,
+        scratch_shapes=[pltpu.VMEM((NDEV * SEQ + 8, DM), F32), pltpu.VMEM((vocab + 8, DM), F32),
+                        pltpu.SemaphoreType.DMA, pltpu.SemaphoreType.DMA((16,))],
+        compiler_params=pltpu.CompilerParams(vmem_limit_bytes=60 * 2**20),
+        name="embed_all",
+    )(keys, starts, dx.reshape(NDEV * SEQ, DM), qkv, dw)
 
 
 def solution(mesh):
     def local_step(tokens, embed_shard, gain_shard, wq_shard, wk_shard, wv_shard, d_query, d_key, d_value):
         vocab_local = embed_shard.shape[0]
         dev_index = lax.axis_index(AXIS_NAME)
-        w_shard = jnp.concatenate([wq_shard, wk_shard, wv_shard], axis=1).astype(BF16)
-        d_own = jnp.concatenate([d_query[0], d_key[0], d_value[0]], axis=1)
-        gain_pad = jnp.pad(gain_shard[None], ((0, 0), (0, 128 - WROWS)))
-        tok_all, gain_all, w_all, d_all = gather_all(tokens, gain_pad, w_shard, d_own)
-        gain_full = gain_all[:, 0, :WROWS].reshape(1, DM)
-        w_full = w_all.reshape(DM, DF)
+        tok_all, gain_all, w_all, d_all, part_rows = gather_all(
+            tokens, gain_shard[None], (wq_shard, wk_shard, wv_shard), (d_query[0], d_key[0], d_value[0]), embed_shard)
+        gain_full = gain_all.reshape(1, DM)
         local_ids = tok_all[:, 0, :] - dev_index * vocab_local
         is_owned = (local_ids >= 0) & (local_ids < vocab_local)
-        owned_rows = jnp.take(embed_shard, jnp.where(is_owned, local_ids, 0), axis=0).astype(BF16)
-        part_rows = jnp.where(is_owned[:, :, None], owned_rows, jnp.zeros((), BF16))
-        qkv, dx_all, dw, dgain = step_all(part_rows, d_all, w_full, gain_full, d_own)
-        scatter_ids = jnp.where(is_owned, local_ids, vocab_local)
-        d_embed = jnp.zeros(embed_shard.shape, F32).at[scatter_ids].add(dx_all, mode="drop")
+        qkv, dx_all, dw, dgain = step_all(part_rows, d_all, w_all.reshape(DM, DF), gain_full)
+        d_embed, *small = embed_all(local_ids, is_owned, dx_all, qkv, dw, vocab_local)
         d_norm_gain = lax.dynamic_slice(dgain, (0, dev_index * WROWS), (1, WROWS))[0]
-        return (qkv[None, :, :DM], qkv[None, :, DM:DM + 128], qkv[None, :, DM + 128:], d_embed, d_norm_gain,
-                dw[:, :DM], dw[:, DM:DM + 128], dw[:, DM + 128:])
+        return (*(a[None] for a in small[:3]), d_embed, d_norm_gain, *small[3:])
 
     row_spec = P(AXIS_NAME, None)
     act_spec = P(AXIS_NAME, None, None)

time: 210 us -> 156 us (0.74)
  other arithmetic: 63.3 us -> 8.83 us
  local copies, waits for them, and re-layouts: 40.6 us -> 2.48 us
  Pallas kernels: 105 us -> 143 us
    scatter-add x1 -> x0, other arithmetic: 50.2 us -> none  [local_step(): jnp.zeros(embed_shard.shape, F32).at[scatter_ids].add(dx_all, mode='drop')]
    gather x1 -> x0, local copies, waits for them, and re-layouts: 30.4 us -> none  [local_step(): jnp.take(embed_shard, jnp.where(is_owned, local_ids, 0), axis=0)]
    pallas_call x0 -> x1, Pallas kernels: none -> 28.4 us  [embed_all(): pl.pallas_call(embed_kernel, out_shape=(sds((vocab, DM), F32), sds((SEQ,...]
    pallas_call x1, Pallas kernels: 48.3 us -> 58.8 us  [gather_all(): pl.pallas_call(gather_kernel, out_shape=(jax.ShapeDtypeStruct((NDEV, 1, S...]
    select_n x3 -> x1, other arithmetic: 8.06 us -> 0.08 us  [embed_all(): starts = jnp.concatenate([(below[:1] + 7) // 8, below[1:] // 8])]
    sort x0 -> x1, other arithmetic: none -> 5.78 us  [embed_all(): jnp.sort(jnp.where(is_owned, local_ids, vocab).reshape(-1) * 4096 + order)]
    slice x3 -> x0, local copies, waits for them, and re-layouts: 3.73 us -> none  [the longest x1 1.62 us: local_step(): dw[:, :DM]]
    broadcast_in_dim x2 -> x0, local copies, waits for them, and re-layouts: 3.35 us -> none  [the longest x1 1.82 us: local_step(): qkv[None, :, :DM]]
where the time goes in v2:
time: 156 us; the launch traced here: 155 us
  Pallas kernels  143 us (92%)
  other arithmetic  8.83 us (6%)
  local copies, waits for them, and re-layouts  2.48 us (2%)
    pallas_call x1, Pallas kernels, gather_all(): pl.pallas_call(gather_kernel, out_shape=(jax.ShapeDtypeStruct((NDEV, 1, S...  58.8 us
    pallas_call x1, Pallas kernels, step_all(): pl.pallas_call(step_kernel, out_shape=(jax.ShapeDtypeStruct((SEQ, DF), BF...  55.9 us
    pallas_call x1, Pallas kernels, embed_all(): pl.pallas_call(embed_kernel, out_shape=(sds((vocab, DM), F32), sds((SEQ,...  28.4 us
    sort x1, other arithmetic, embed_all(): jnp.sort(jnp.where(is_owned, local_ids, vocab).reshape(-1) * 4096 + order)  5.78 us

profile of v2, /device:TPU:0, one launch (start us, length us, event | category | flops | bytes accessed | tf_op | source)
XLA Modules:
  0.0 155.2 jit_solution(13406464842952929000)
XLA Ops:
  0.6 0.0 copy-start.1
  0.7 58.8 %gather_all.1 = (s32[16,1,256]{2,1,0:T(1,128)}, f32[16,1,56]{2,1,0:T(1,128)}, bf16[16,56,1152]{2,1,0:T(8,128)(2,1)}, bf16[16,256,1152]{2,1,0:T(8,128)(2,1)}, bf16[16,256,896]{2,1,0:T(8,128)(2,1)}) custom-call(s32[1,256]{1,0:T(1,128)} %tok.1, f32[1,56]{1,0:T(1,128)} %bitcast.22, f32[56,896]{1,0:T(8,128)} %wq.1, f32[56,128]{1,0:T(8,128)} %wk.1, f32[56,128]{1,0:T(8,128)} %wv.1, ...), custom_call_target="tpu_custom_call" | custom-call | tf_op jit(solution)/shard_map/gather_all/pallas_call | solution.py:171
  59.5 0.7 broadcast_subtract_fusion
  60.2 5.8 %sort.14 = (s32[4096]{0:T(1024)S(1)}, s32[4096]{0:T(1024)}) sort(s32[4096]{0:T(1024)S(1)} %iota_add_fusion, s32[4096]{0:T(1024)S(1)} %iota.7), dimensions={0}, to_apply=%region_0.1 | sort | flops 49152 | bytes 65536 | tf_op jit(solution)/shard_map/jit(sort)/sort | solution.py:417
  66.0 0.0 copy-start
  66.0 0.0 copy-done.1
  66.0 0.2 convert_reduce_fusion
  66.3 0.1 and_select_fusion
  66.4 0.6 pad_add_fusion.starts
  67.0 0.5 broadcast.33
  67.5 1.4 reduce.3
  68.9 0.7 reshape.37.gain
  69.6 55.9 %step_all.1 = (bf16[256,1152]{1,0:T(8,128)(2,1)}, f32[16,256,896]{2,1,0:T(8,128)}, f32[56,1152]{1,0:T(8,128)}, f32[8,896]{1,0:T(8,128)}) custom-call(bf16[16,256,896]{2,1,0:T(8,128)(2,1)} %get-tuple-element.28.xp, bf16[16,256,1152]{2,1,0:T(8,128)(2,1)} %get-tuple-element.29.g, bf16[896,1152]{1,0:T(8,128)(2,1)} %bitcast.16, f32[1,896]{1,0:T(1,128)} %reshape.37.gain), custom_call_target="tpu_custom_call" | custom-call | tf_op jit(solution)/shard_map/step_all/pallas_call | solution.py:349
  125.5 1.3 dynamic-slice_bitcast_fusion
  126.8 0.0 copy-done
  126.8 28.4 %embed_all.1 = (f32[9496,896]{1,0:T(8,128)}, bf16[256,896]{1,0:T(8,128)(2,1)}, bf16[256,128]{1,0:T(8,128)(2,1)}, bf16[256,128]{1,0:T(8,128)(2,1)}, f32[56,896]{1...) custom-call(s32[4096]{0:T(1024)} %copy-done, s32[17]{0:T(128)} %pad_add_fusion.starts, f32[4096,896]{1,0:T(8,128)} %bitcast.15, ...), custom_call_target="tpu_custom_call" | custom-call | tf_op jit(solution)/shard_map/embed_all/pallas_call | solution.py:425
  (2 shorter events, 0.0 us)
Async XLA Ops:
  0.6 65.3 %copy-start.1 = (s32[17]{0:T(128)S(1)}, s32[17]{0:T(128)}, u32[]{:S(2)}) copy-start(s32[17]{0:T(128)} %constant.65) | copy-start | bytes 208
  66.0 60.8 %copy-start = (s32[4096]{0:T(1024)}, s32[4096]{0:T(1024)S(1)}, u32[]{:S(2)}) copy-start(s32[4096]{0:T(1024)S(1)} %get-tuple-element.27.keys) | copy-start | bytes 49156

commit v3 on v1

v3 whole, which is shorter than its diff:
```python
import functools
import jax
import jax.numpy as jnp
from jax import lax
from jax.experimental import pallas as pl
from jax.experimental.pallas import tpu as pltpu
from jax.sharding import PartitionSpec as P

AXIS_NAME = "fsdp"
NDEV = 16
STRIDES = (2, 4, 8)
MESH = pl.DeviceIdType.MESH
SEQ = 256
DM = 896
DF = 1152
WROWS = 56
PAIR = 2
STEP = PAIR * SEQ
CHUNK = 64
QUARTERS = 4
SPLIT = 18
F32 = jnp.float32
BF16 = jnp.bfloat16


def flip(me, stride):
    return me + stride * (1 - 2 * ((me // stride) % 2))


def flip_mask(me, mask, order=(0, 1, 2)):
    for pos in range(3):
        if (mask >> pos) & 1:
            me = flip(me, STRIDES[order[pos]])
    return me


def colour_order(c):
    return (c, (c + 1) % 3, (c + 2) % 3)


def remote(src, dst, send, recv, dev):
    return pltpu.make_async_remote_copy(src_ref=src, dst_ref=dst, send_sem=send, recv_sem=recv,
                                        device_id=(dev,), device_id_type=MESH)


def barrier_all(me):
    sem = pltpu.get_barrier_semaphore()
    for k in range(1, NDEV):
        pl.semaphore_signal(sem, inc=1, device_id=((me + k) % NDEV,), device_id_type=MESH)
    pl.semaphore_wait(sem, NDEV - 1)


class Gather:
    def __init__(self, me, src, dst, sems, width):
        self.me, self.src, self.dst, self.width = me, src, dst, width
        self.send, self.recv, self.csend, self.crecv = sems

    def cols(self, c):
        return pl.ds(c * self.width, self.width)

    def block(self, c, mask, base=None):
        origin = flip_mask(self.me if base is None else base, mask, colour_order(c))
        return self.dst.at[origin, :, self.cols(c)]

    def link_copy(self, c, mask, pos):
        src = self.src.at[:, self.cols(c)] if mask == 0 else self.block(c, mask)
        new = mask | (1 << pos)
        return remote(src, self.block(c, mask), self.send.at[c, new], self.recv.at[c, new],
                      flip(self.me, STRIDES[colour_order(c)[pos]]))

    def core_copy(self, c, mask):
        src = self.src.at[:, self.cols(c)] if mask == 0 else self.block(c, mask)
        return remote(src, self.block(c, mask), self.csend.at[c, mask], self.crecv.at[c, mask], flip(self.me, 1))

    def start_piece(self, c, mask):
        for pos in range(mask.bit_length(), 3):
            self.link_copy(c, mask, pos).start()
        self.core_copy(c, mask).start()

    def wait_piece(self, c, mask):
        pos = mask.bit_length() - 1
        self.link_copy(c, mask & ~(1 << pos), pos).wait_recv()

    def finish(self):
        for c in range(3):
            for mask in range(8):
                for pos in range(mask.bit_length(), 3):
                    self.link_copy(c, mask, pos).wait_send()
                self.core_copy(c, mask).wait()


def rotate(x, amount, axis):
    extent = x.shape[axis]
    return jnp.concatenate([lax.slice_in_dim(x, extent - amount, extent, axis=axis),
                            lax.slice_in_dim(x, 0, extent - amount, axis=axis)], axis=axis)


class Scatter:
    def __init__(self, me, part, acc, bufs, sems, piece):
        self.me, self.part, self.acc, self.piece = me, part, acc, piece
        self.r0, self.r = bufs[0], bufs[1:]
        self.csend, self.crecv, self.send, self.recv = sems

    def core_copy(self, mask):
        block = flip_mask(flip(self.me, 1), mask)
        return remote(self.part(block), self.r0.at[mask], self.csend.at[mask], self.crecv.at[mask], flip(self.me, 1))

    def phase_copy(self, c, phase, rel):
        order = colour_order(c)
        absmask = sum(1 << order[pos] for pos in range(3) if (rel >> pos) & 1)
        low = rel >> (phase + 1)
        sem = (0, 4, 6)[phase] + low
        return remote(self.piece(self.acc.at[absmask], c), self.piece(self.r[phase].at[low], c),
                      self.send.at[c, sem], self.recv.at[c, sem], flip(self.me, STRIDES[order[phase]]))

    def core_start(self):
        for mask in range(7, -1, -1):
            self.core_copy(mask).start()

    def core_done(self, mask):
        self.core_copy(mask).wait_recv()
        self.acc[mask] = self.part(flip_mask(self.me, mask))[...] + self.r0[mask]
        for c in range(3):
            if (mask >> c) & 1:
                order = colour_order(c)
                rel = sum(1 << pos for pos in range(3) if (mask >> order[pos]) & 1)
                self.phase_copy(c, 0, rel).start()

    def phase_done(self, c, phase, low):
        order = colour_order(c)
        rel = low << (phase + 1)
        self.phase_copy(c, phase, rel | (1 << phase)).wait_recv()
        absmask = sum(1 << order[pos] for pos in range(3) if (rel >> pos) & 1)
        dst = self.piece(self.acc.at[absmask], c)
        dst[...] = dst[...] + self.piece(self.r[phase].at[low], c)[...]

    def move_on(self, c, phase, rel):
        self.phase_copy(c, phase, rel).start()

    def steps(self):
        out = [functools.partial(self.core_done, mask) for mask in range(7, -1, -1)]

        def phase0(c, low):
            self.phase_done(c, 0, low)
            if low & 1:
                self.move_on(c, 1, low << 1)

        def phase1(c, low):
            self.phase_done(c, 1, low)
            if low & 1:
                self.move_on(c, 2, low << 2)

        for low in (3, 1, 2, 0):
            out += [functools.partial(phase0, c, low) for c in range(3)]
        for low in (1, 0):
            out += [functools.partial(phase1, c, low) for c in range(3)]
        out += [functools.partial(self.phase_done, c, 2, 0) for c in range(3)]
        return out

    def finish(self):
        for mask in range(8):
            self.core_copy(mask).wait_send()
        for c in range(3):
            for phase in range(3):
                for low in range(4 >> phase):
                    self.phase_copy(c, phase, (low << (phase + 1)) | (1 << phase)).wait_send()


ROW_PIECES = ((0, 96), (96, 80), (176, 80))


def row_piece(ref, c):
    start, size = ROW_PIECES[c]
    return ref.at[pl.ds(start, size)]


def col_piece(ref, c):
    return ref.at[:, pl.ds(c * (DF // 3), DF // 3)]


def step_kernel(tok, gain, wq, wk, wv, dq, dk, dv, table, tok_o, w_o, g, qkv_o, dx_o, dw_o, dg_o,
                wpad, d, ids, tok_v, tok_row, gain_p, gain_v, gain8, rows, xp, xacc, x0, x1, x2, x3, w0, w1, w2, w3, dgp, dgsum, dgall,
                tabsem, loc, gsem, dxsem, small_send, small_recv, dgs, dgr, gws, gwr, gwcs, gwcr, gds, gdr, gdcs, gdcr,
                xcs, xcr, xs, xr, wcs, wcr, ws, wr):
    me = lax.axis_index(AXIS_NAME)
    vocab = table.shape[0]
    tiles = DM // 128
    for ref, src in ((wpad, (wq, wk, wv)), (d, (dq, dk, dv))):
        height = src[0].shape[0]
        ref[:height, :DM] = src[0][...].astype(BF16)
        ref[:height, DM:DM + 128] = src[1][...].astype(BF16)
        ref[:height, DM + 128:] = src[2][...].astype(BF16)
    w = wpad.at[pl.ds(0, WROWS)]
    gain_p[...] = jnp.zeros_like(gain_p)
    gain_p[0:1, 0:WROWS] = gain[...]
    gain_v[...] = jnp.zeros_like(gain_v)
    gain_v[me] = gain_p[...]
    dgall[...] = jnp.zeros_like(dgall)
    dgp[...] = jnp.zeros_like(dgp)
    tok_v[me] = tok[...]
    wg = Gather(me, w, WRows(w_o), (gws, gwr, gwcs, gwcr), DF // 3)
    dg = Gather(me, d, g, (gds, gdr, gdcs, gdcr), DF // 3)
    xrs = Scatter(me, lambda b: xp.at[b], xacc, (x0, x1, x2, x3), (xcs, xcr, xs, xr), row_piece)
    own = [pltpu.make_async_copy(w, w_o.at[pl.ds(pl.multiple_of(me * WROWS, 8), WROWS)], loc.at[0]),
           pltpu.make_async_copy(d, g.at[me], loc.at[1])]
    tok_copies, gain_copies = [], []
    for k in range(1, NDEV):
        dev = (me + k) % NDEV
        tok_copies.append(remote(tok, tok_v.at[me], small_send.at[0, k], small_recv.at[0, k], dev))
        gain_copies.append(remote(gain_p.at[pl.ds(0, 1)], gain_v.at[me, pl.ds(0, 1)], small_send.at[1, k], small_recv.at[1, k], dev))

    def piece(gather, c, mask):
        gather.wait_piece(c, mask)
        gather.start_piece(c, mask)

    def pieces(mask):
        return [functools.partial(piece, gather, c, mask) for gather in (wg, dg) for c in range(3)]

    def gather_rows(tab):
        table_copies = [pltpu.make_async_copy(table.at[:, pl.ds(s * 128, 128)], tab.at[pl.ds(0, vocab), s], tabsem.at[s])
                        for s in range(tiles)]
        for copy in table_copies:
            copy.start()
        tab[vocab] = jnp.zeros((8, 128), F32)
        barrier_all(me)
        for copy in tok_copies + gain_copies:
            copy.start()
        for gather in (wg, dg):
            for c in range(3):
                gather.start_piece(c, 0)
        for copy in own:
            copy.start()
        for copy in tok_copies:
            copy.wait()
        local = tok_v[...] - me * vocab
        tok_row[...] = jnp.where((local >= 0) & (local < vocab), local, vocab)
        ids_copy = pltpu.make_async_copy(tok_row, ids, loc.at[2])
        ids_copy.start()
        tok_o[...] = tok_v[...]
        for copy in gain_copies:
            copy.wait()
        total = jnp.zeros((8, DM), F32)
        for k in range(NDEV):
            wide = jnp.concatenate([gain_v[k], jnp.zeros((8, DM - 128), F32)], axis=1)
            total = total + (rotate(wide, k * WROWS, 1) if k else wide)
        gain8[...] = total
        ids_copy.wait()
        for copy in table_copies:
            copy.wait()
        for event in pieces(1):
            event()
        when = {2: pieces(2), 7: pieces(3)[:3], 9: pieces(3)[3:]}

        @pl.loop(0, NDEV)
        def _(k):
            base = me + (1 - k // 8) * (1 - 2 * (me % 2))
            mask = 7 - k % 8
            b = base
            for bit, stride in enumerate(STRIDES):
                b = b + stride * (1 - 2 * ((base // stride) % 2)) * ((mask // (1 << bit)) % 2)

            @pl.loop(0, SEQ // 16)
            def _(i):
                for j in range(16):
                    rows[i * 16 + j] = tab[ids[b, 0, i * 16 + j]]

            for s in range(tiles):
                xp[b, :, s * 128:(s + 1) * 128] = rows[:, s, :].astype(BF16)
            for at in range(NDEV):
                group = when.get(at, [])
                if at >= 1 and at <= 8:
                    group = [lambda at=at: xrs.core_copy(8 - at).start()] + group
                if group:
                    @pl.when(k == at)
                    def _(group=group):
                        for event in group:
                            event()

    pl.run_scoped(gather_rows, pltpu.VMEM((vocab + 1, 8, 128), F32))
    events = xrs.steps()
    for event in events[:8]:
        event()
    for mask in range(4, 8):
        for event in pieces(mask):
            event()
    wg.finish()
    dg.finish()
    for copy in own:
        copy.wait()
    events = events[8:]

    def finish_step(wfull, gbuf, dxbuf, dwp, wacc):
        load = lambda t, slot: pltpu.make_async_copy(g.at[pl.ds(PAIR * t, PAIR)], gbuf.at[slot], gsem.at[slot])
        store = lambda t, slot: pltpu.make_async_copy(dxbuf.at[slot], dx_o.at[pl.ds(STEP * t, STEP)], dxsem.at[slot])
        w_copy = pltpu.make_async_copy(w_o, wfull, loc.at[3])
        w_copy.start()
        load(0, 0).start()
        part = lambda b: dwp.at[pl.ds(pl.multiple_of(b * WROWS, 8), WROWS)]
        wrs = Scatter(me, part, wacc, (w0, w1, w2, w3), (wcs, wcr, ws, wr), col_piece)

        def weight_grads():
            x = xacc[0].astype(F32)
            r = lax.rsqrt(jnp.mean(x * x, axis=-1, keepdims=True) + 1e-5)
            n = (x * r * gain8[...][0:1]).astype(BF16)
            dwp[...] = lax.dot_general(n, d[...], (((0,), (0,)), ((), ())), preferred_element_type=F32)
            wrs.core_start()
            qkv_o[...] = jnp.dot(n, wfull[...], preferred_element_type=F32).astype(BF16)

        slots = NDEV // PAIR * QUARTERS
        groups = [events[len(events) * k // SPLIT:len(events) * (k + 1) // SPLIT] for k in range(SPLIT)] + [[weight_grads]]
        later = wrs.steps()
        rest = slots - SPLIT - 1
        groups += [later[len(later) * k // rest:len(later) * (k + 1) // rest] for k in range(rest)]
        w_copy.wait()

        @pl.loop(0, NDEV // PAIR)
        def _(t):
            slot = t % 2

            @pl.when(t + 1 < NDEV // PAIR)
            def _():
                load(t + 1, 1 - slot).start()

            load(t, slot).wait()

            @pl.when(t >= 2)
            def _():
                store(t - 2, slot).wait()

            dxbuf[slot] = lax.dot_general(gbuf[slot].reshape(STEP, DF), wfull[...], (((1,), (1,)), ((), ())),
                                          preferred_element_type=F32)

            def chunk(q):
                at = pl.ds(pl.multiple_of(q * CHUNK, CHUNK), CHUNK)
                dn = dxbuf[slot, at]
                per = SEQ // CHUNK
                x = xp[PAIR * t + q // per, pl.ds(pl.multiple_of((q % per) * CHUNK, CHUNK), CHUNK)].astype(F32)
                r = lax.rsqrt(jnp.mean(x * x, axis=-1, keepdims=True) + 1e-5)
                h = x * r
                dgp[...] += jnp.sum((dn * h).reshape(CHUNK // 8, 8, DM), axis=0)
                u = dn * gain8[...][0:1]
                dxbuf[slot, at] = r * (u - h * jnp.mean(u * h, axis=-1, keepdims=True))

            for part_of in range(QUARTERS):
                pl.loop(part_of * (STEP // CHUNK) // QUARTERS, (part_of + 1) * (STEP // CHUNK) // QUARTERS)(chunk)
                for step in range(NDEV // PAIR):
                    group = groups[step * QUARTERS + part_of]
                    if group:
                        @pl.when(t == step)
                        def _(group=group):
                            for event in group:
                                event()

            store(t, slot).start()

        dgsum[...] = jnp.broadcast_to(jnp.sum(dgp[...], axis=0, keepdims=True), dgsum.shape)
        dgall[me] = dgsum[...]
        small = [remote(dgsum.at[pl.ds(0, 1)], dgall.at[me, pl.ds(0, 1)], dgs.at[k], dgr.at[k], (me + k) % NDEV)
                 for k in range(1, NDEV)]
        for copy in small:
            copy.start()
        dw_o[...] = wacc[0]
        for copy in small:
            copy.wait()
        dg_o[...] = jnp.sum(dgall[...], axis=0)
        store(NDEV // PAIR - 2, 0).wait()
        store(NDEV // PAIR - 1, 1).wait()
        wrs.finish()

    vmem = pltpu.VMEM
    pl.run_scoped(finish_step, vmem((DM, DF), BF16), vmem((2, PAIR, SEQ, DF), BF16), vmem((2, STEP, DM), F32),
                  vmem((DM, DF), F32), vmem((8, WROWS, DF), F32))
    xrs.finish()


class WRows:
    def __init__(self, ref):
        self.ref = ref

    @property
    def at(self):
        return self

    def __getitem__(self, index):
        device, _, cols = index
        return self.ref.at[pl.ds(pl.multiple_of(device * WROWS, 8), WROWS), cols]


def step_all(tok, gain, weights, grads, table):
    vm = pl.BlockSpec(memory_space=pltpu.VMEM)
    hbm = pl.BlockSpec(memory_space=pl.ANY)
    dma = pltpu.SemaphoreType.DMA
    vmem = pltpu.VMEM
    sds = jax.ShapeDtypeStruct
    xb = lambda k: vmem((k, SEQ, DM), BF16)
    wb = lambda k: vmem((k, WROWS, DF), F32)
    return pl.pallas_call(
        step_kernel,
        out_shape=(sds((NDEV, 1, SEQ), jnp.int32), sds((DM, DF), BF16), sds((NDEV, SEQ, DF), BF16), sds((SEQ, DF), BF16),
                   sds((NDEV * SEQ, DM), F32), sds((WROWS, DF), F32), sds((8, DM), F32)),
        in_specs=[vm] * 8 + [hbm],
        out_specs=(vm, hbm, hbm, vm, hbm, vm, vm),
        scratch_shapes=[vmem((64, DF), BF16), vmem((SEQ, DF), BF16), pltpu.SMEM((NDEV, 1, SEQ), jnp.int32),
                        vmem((NDEV, 1, SEQ), jnp.int32), vmem((NDEV, 1, SEQ), jnp.int32), vmem((8, 128), F32), vmem((NDEV, 8, 128), F32), vmem((8, DM), F32),
                        vmem((SEQ, 8, 128), F32), xb(NDEV), xb(8), xb(8), xb(4), xb(2), xb(1), wb(8), wb(4), wb(2), wb(1),
                        vmem((8, DM), F32), vmem((8, DM), F32), vmem((NDEV, 8, DM), F32),
                        dma((8,)), dma((4,)), dma((2,)), dma((2,)), dma((2, NDEV)), dma((2, NDEV)), dma((NDEV,)), dma((NDEV,))]
        + [dma((3, 8))] * 8 + [dma((8,)), dma((8,)), dma((3, 7)), dma((3, 7))] * 2,
        compiler_params=pltpu.CompilerParams(collective_id=0, has_side_effects=True, vmem_limit_bytes=67043328),
        name="step_all",
    )(tok, gain, *weights, *grads, table)


def embed_kernel(keys, starts, dx, qkv, dw, dg, de_o, q_o, k_o, v_o, dwq_o, dwk_o, dwv_o, dg_o, dxv, de, insem, outsem):
    vocab = de_o.shape[0]
    fetch = pltpu.make_async_copy(dx, dxv.at[pl.ds(0, NDEV * SEQ)], insem)
    fetch.start()

    @pl.loop(0, (vocab + 8) // 32)
    def _(i):
        de[pl.ds(pl.multiple_of(i * 32, 32), 32)] = jnp.zeros((32, DM), F32)

    for outs, ref in (((q_o, k_o, v_o), qkv), ((dwq_o, dwk_o, dwv_o), dw)):
        outs[0][...] = ref[:, :DM]
        outs[1][...] = ref[:, DM:DM + 128]
        outs[2][...] = ref[:, DM + 128:]
    dg_o[...] = dg[...][0:1]
    fetch.wait()
    top = starts[0, 0] - 1

    def token(p, carry):
        prev, total = carry
        key = keys[p]
        row = lax.shift_right_logical(key, 12)
        total = jnp.where(row == prev, total, 0.0) + dxv[pl.ds(key & 4095, 1), :]
        de[pl.ds(row, 1), :] = total
        return row, total

    def group(i, carry):
        first = (top - i) * 8
        for j in range(7, -1, -1):
            carry = token(first + j, carry)
        return carry

    def two_groups(i, carry):
        return group(2 * i + 1, group(2 * i, carry))

    carry = (jnp.int32(-1), jnp.zeros((1, DM), F32))
    done = jnp.int32(0)
    copies = []
    bounds = embed_bounds(vocab)
    for k in range(len(bounds) - 1):
        low, high = bounds[k + 1], bounds[k]
        upto = top + 1 - starts[0, k + 1]
        even = lax.shift_right_logical(done + 1, 1)
        carry = lax.fori_loop(done, jnp.minimum(even * 2, upto), group, carry)
        last = jnp.maximum(lax.shift_right_logical(upto, 1), even)
        carry = lax.fori_loop(even, last, two_groups, carry)
        carry = lax.fori_loop(jnp.maximum(last * 2, done), upto, group, carry)
        done = upto
        copies.append(pltpu.make_async_copy(de.at[pl.ds(low, high - low)], de_o.at[pl.ds(low, high - low)], outsem.at[k]))
        copies[-1].start()
    for copy in copies:
        copy.wait()


def embed_bounds(vocab):
    blocks = 16
    return [vocab] + [(vocab * k // blocks) // 8 * 8 for k in range(blocks - 1, 0, -1)] + [0]


def embed_all(local, dx, qkv, dw, dg, vocab):
    order = jnp.arange(NDEV * SEQ, dtype=jnp.int32)
    keys = jnp.sort(jnp.where((local >= 0) & (local < vocab), local, vocab).reshape(-1) * 4096 + order)
    bounds = jnp.array(embed_bounds(vocab), jnp.int32)
    below = jnp.sum((keys[None, :] < bounds[:, None] * 4096).astype(jnp.int32), axis=1)
    starts = jnp.concatenate([(below[:1] + 7) // 8, below[1:] // 8])[None]
    vm = pl.BlockSpec(memory_space=pltpu.VMEM)
    hbm = pl.BlockSpec(memory_space=pl.ANY)
    smem = pl.BlockSpec(memory_space=pltpu.SMEM)
    sds = jax.ShapeDtypeStruct
    dma = pltpu.SemaphoreType.DMA
    return pl.pallas_call(
        embed_kernel,
        out_shape=(sds((vocab, DM), F32), sds((SEQ, DM), BF16), sds((SEQ, 128), BF16), sds((SEQ, 128), BF16),
                   sds((WROWS, DM), F32), sds((WROWS, 128), F32), sds((WROWS, 128), F32), sds((1, WROWS), F32)),
        in_specs=[smem, smem, hbm, vm, vm, vm],
        out_specs=(hbm,) + (vm,) * 7,
        scratch_shapes=[pltpu.VMEM((NDEV * SEQ + 8, DM), F32), pltpu.VMEM((vocab + 8, DM), F32), dma, dma((16,))],
        compiler_params=pltpu.CompilerParams(vmem_limit_bytes=62 * 2**20),
        name="embed_all",
    )(keys, starts, dx, qkv, dw, dg)


def solution(mesh):
    def local_step(tokens, embed_shard, gain_shard, wq_shard, wk_shard, wv_shard, d_query, d_key, d_value):
        vocab_local = embed_shard.shape[0]
        tok_all, _, _, qkv, dx_all, dw, dgain = step_all(
            tokens, gain_shard[None], (wq_shard, wk_shard, wv_shard), (d_query[0], d_key[0], d_value[0]), embed_shard)
        dgain = lax.dynamic_slice(dgain, (0, lax.axis_index(AXIS_NAME) * WROWS), (8, WROWS))
        d_embed, *small = embed_all(tok_all - lax.axis_index(AXIS_NAME) * vocab_local, dx_all, qkv, dw, dgain, vocab_local)
        return (*(a[None] for a in small[:3]), d_embed, small[6][0], *small[3:6])

    row_spec = P(AXIS_NAME, None)
    act_spec = P(AXIS_NAME, None, None)
    vec_spec = P(AXIS_NAME)
    return jax.shard_map(local_step, mesh=mesh,
                         in_specs=(row_spec, row_spec, vec_spec, row_spec, row_spec, row_spec, act_spec, act_spec, act_spec),
                         out_specs=(act_spec, act_spec, act_spec, row_spec, vec_spec, row_spec, row_spec, row_spec),
                         check_vma=False)
```

time: 210 us -> 147 us (0.70)
  other arithmetic: 63.3 us -> 8.81 us
  local copies, waits for them, and re-layouts: 40.6 us -> 1.97 us
  Pallas kernels: 105 us -> 135 us
    scatter-add x1 -> x0, other arithmetic: 50.2 us -> none  [local_step(): jnp.zeros(embed_shard.shape, F32).at[scatter_ids].add(dx_all, mode='drop')]
    gather x1 -> x0, local copies, waits for them, and re-layouts: 30.4 us -> none  [local_step(): jnp.take(embed_shard, jnp.where(is_owned, local_ids, 0), axis=0)]
    pallas_call x2, Pallas kernels: 105 us -> 135 us  [the longest x1 106 us: step_all(): pl.pallas_call(step_kernel, out_shape=(sds((NDEV, 1, SEQ), jnp.int32), sd...]
    select_n x3 -> x1, other arithmetic: 8.06 us -> 0.08 us  [embed_all(): starts = jnp.concatenate([(below[:1] + 7) // 8, below[1:] // 8])[None]]
    sort x0 -> x1, other arithmetic: none -> 6.5 us  [embed_all(): jnp.sort(jnp.where((local >= 0) & (local < vocab), local, vocab).reshape(...]
    slice x3 -> x0, local copies, waits for them, and re-layouts: 3.73 us -> none  [the longest x1 1.62 us: local_step(): dw[:, :DM]]
    broadcast_in_dim x2 -> x0, local copies, waits for them, and re-layouts: 3.35 us -> none  [the longest x1 1.82 us: local_step(): qkv[None, :, :DM]]
    concatenate x2 -> x0, other arithmetic: 2.62 us -> none  [the longest x1 1.96 us: local_step(): d_own = jnp.concatenate([d_query[0], d_key[0], d_value[0]], axis=1)]
where the time goes in v3:
time: 147 us; the launch traced here: 146 us
  Pallas kernels  135 us (92%)
  other arithmetic  8.81 us (6%)
  local copies, waits for them, and re-layouts  1.97 us (1%)
    pallas_call x1, Pallas kernels, step_all(): pl.pallas_call(step_kernel, out_shape=(sds((NDEV, 1, SEQ), jnp.int32), sd...  106 us
    pallas_call x1, Pallas kernels, embed_all(): pl.pallas_call(embed_kernel, out_shape=(sds((vocab, DM), F32), sds((SEQ,...  28.3 us
    sort x1, other arithmetic, embed_all(): jnp.sort(jnp.where((local >= 0) & (local < vocab), local, vocab).reshape(...  6.5 us

profile of v3, /device:TPU:0, one launch (start us, length us, event | category | flops | bytes accessed | tf_op | source)
XLA Modules:
  0.0 146.3 jit_solution(5153823729433567740)
XLA Ops:
  0.6 0.6 iota.7
  1.2 106.5 %step_all.1 = (s32[16,1,256]{2,1,0:T(1,128)}, bf16[896,1152]{1,0:T(8,128)(2,1)}, bf16[16,256,1152]{2,1,0:T(8,128)(2,1)}, bf16[256,1152]{1,0:T(8,128)(2,1)}, f32[...) custom-call(s32[1,256]{1,0:T(1,128)} %tok.1, f32[1,56]{1,0:T(1,128)} %bitcast.16, f32[56,896]{1,0:T(8,128)} %wq.1, ...), custom_call_target="tpu_custom_call" | custom-call | tf_op jit(solution)/shard_map/step_all/pallas_call | solution.py:397
  107.7 0.8 fusion
  108.5 6.5 %sort.14 = (s32[4096]{0:T(1024)S(1)}, s32[4096]{0:T(1024)}) sort(s32[4096]{0:T(1024)S(1)} %iota_add_fusion, s32[4096]{0:T(1024)} %iota.7), dimensions={0}, to_apply=%region_0.1 | sort | flops 49152 | bytes 65536 | tf_op jit(solution)/shard_map/jit(sort)/sort | solution.py:474
  115.0 0.0 copy-start
  115.0 0.9 convert_reduce_fusion
  115.9 0.1 and_select_fusion.1
  116.0 0.6 add_bitcast_fusion.starts
  116.6 1.4 constant_dynamic-slice_fusion.dg
  118.0 0.0 copy-done
  118.0 28.3 %embed_all.1 = (f32[9496,896]{1,0:T(8,128)}, bf16[256,896]{1,0:T(8,128)(2,1)}, bf16[256,128]{1,0:T(8,128)(2,1)}, bf16[256,128]{1,0:T(8,128)(2,1)}, f32[56,896]{1...) custom-call(s32[4096]{0:T(1024)} %copy-done, s32[1,17]{1,0:T(1,128)} %add_bitcast_fusion.starts, ...), custom_call_target="tpu_custom_call" | custom-call | tf_op jit(solution)/shard_map/embed_all/pallas_call | solution.py:483
  (1 shorter events, 0.0 us)
Async XLA Ops:
  115.0 3.0 %copy-start = (s32[4096]{0:T(1024)}, s32[4096]{0:T(1024)S(1)}, u32[]{:S(2)}) copy-start(s32[4096]{0:T(1024)S(1)} %get-tuple-element.24.keys) | copy-start | bytes 49156
